TPU v7x, 32 devices: a whole 2x2x4 slice. The times are simulated.
32 devices in a mesh: gx: 4 (over z), gy: 8 (over y, x, core).
Axes of the slice: x: 2, y: 2, z: 4, core: 2. Of those that a mesh axis runs over, the one named last changes fastest.
Arguments:
- substrates: float32 [8, 256, 128, 128], P(None, 'gx', 'gy'), may hold values from 0 to 2
- uptake: float32 [256, 128, 128], P('gx', 'gy'), may hold values from 0.5 to 2
- diffusion: float32 [8], replicated, may hold values from 0.1 to 0.15
- decay_rate: float32 [8], replicated, may hold values from 0.01 to 0.1
Outputs:
- advanced: float32 [8, 256, 128, 128], P(None, 'gx', 'gy')
All inputs are finite; a program needn't handle non-finite values.
Results may differ from a plain program's by a relative error of at most 0.00002.
Values sent between devices are 32-bit elements; how exact they have to be, the bound alone decides.
A program may use at most 128 MiB of HBM per device.

v0:
```python
import jax
import jax.numpy as jnp
from jax import lax
from jax.sharding import PartitionSpec as P

SUBSTEPS = 4


def padded_2(block, sides, width):
    for axis, dim in sides:
        count = lax.axis_size(axis)
        forward = [(i, i + 1) for i in range(count - 1)]
        forward.append((count - 1, 0))
        backward = [(target, source) for source, target in forward]
        low = lax.ppermute(
            lax.slice_in_dim(block, block.shape[dim] - width, None, axis=dim), axis, forward
        )
        high = lax.ppermute(lax.slice_in_dim(block, 0, width, axis=dim), axis, backward)
        block = jnp.concatenate([low, block, high], axis=dim)
    return block


def advance(padded, inner_uptake, diffuse, decays):
    center = padded[:, 1:-1, 1:-1, :]
    laplace = padded[:, 2:, 1:-1, :] + padded[:, :-2, 1:-1, :]
    laplace = laplace + padded[:, 1:-1, 2:, :] + padded[:, 1:-1, :-2, :]
    laplace = laplace + jnp.roll(center, -1, 3) + jnp.roll(center, 1, 3)
    laplace = laplace - 6.0 * center
    return center + diffuse * laplace - decays * inner_uptake[None] * center


def local(substrates, uptake, diffusion, decay_rate):
    diffuse = diffusion[:, None, None, None]
    decays = decay_rate[:, None, None, None]
    concentration = substrates
    for substep in range(SUBSTEPS):
        padded = padded_2(concentration, (("gx", 1), ("gy", 2)), 1)
        concentration = advance(padded, uptake, diffuse, decays)
    return concentration


def solution(mesh):
    placed = (P(None, "gx", "gy", None), P("gx", "gy", None), P(), P())
    return jax.shard_map(
        local, mesh=mesh, in_specs=placed, out_specs=P(None, "gx", "gy", None), check_vma=False
    )
```

profile of v0, /device:TPU:0, one launch (start us, length us, event | category | flops | bytes accessed | tf_op | source)
XLA Modules:
  0.0 124.5 jit_solution(14442852729455933330)
XLA Ops:
  0.0 4.6 %copy.15 = f32[8,64,16,128]{3,0,2,1:T(8,128)S(1)} copy(f32[8,64,16,128]{3,2,1,0:T(8,128)} %param.4) | data formatting | bytes 8388608 | tf_op args[0]
  4.6 5.1 %collective-permute-start = (f32[8,1,16,128]{3,0,2,1:T(8,128)S(1)}, f32[8,1,16,128]{3,0,2,1:T(8,128)S(1)}, u32[]{:S(2)}, u32[]{:S(2)}) collective-permute-start(f32[8,1,16,128]{3,0,2,1:T(8,128)S(1)} %get-tuple-element.35), channel_id=1, source_target_pairs={{8,0},{16,8},{24,16},{0,24},{9,1},{17,9},{25,17},{1,25},{10,2},{18... | collective-permute-start | bytes 196616 | tf_op jit(solution)/shard_map/ppermute | solution.py:18
  9.8 4.8 %fusion.47 = (f32[8,64,16,127]{3,0,2,1:T(8,128)}, f32[8,64,16,127]{3,0,2,1:T(8,128)}) fusion(f32[8,64,16,128]{3,0,2,1:T(8,128)S(1)} %copy.15), kind=kLoop, calls=%fused_computation.91 | loop fusion | bytes 16646144 | tf_op jit(solution)/shard_map/jit(_roll_static)/slice | solution.py:27
  14.6 1.2 collective-permute-done.1
  15.8 2.4 %constant_dynamic-update-slice_fusion.1 = f32[8,66,16,128]{3,0,2,1:T(8,128)S(1)} fusion(f32[8,66,16,128]{3,0,2,1:T(8,128)S(1)} %constant_dynamic-update-slice_fusion.2, f32[8,64,16,128]{3,2,1,0:T(8,128)S(1)} %copy-done), kind=kLoop, calls=%fused_computation.78 | loop fusion | bytes 8388608
  18.4 0.5 collective-permute-start.2
  18.9 5.0 %fusion.46 = (f32[8,64,16,1]{3,0,2,1:T(8,128)}, f32[8,64,16,1]{3,0,2,1:T(8,128)}) fusion(f32[8,64,16,128]{3,0,2,1:T(8,128)S(1)} %copy.15), kind=kLoop, calls=%fused_computation.90 | loop fusion | bytes 131072 | tf_op jit(solution)/shard_map/jit(_roll_static)/slice | solution.py:27
  23.9 1.1 collective-permute-done.2
  25.0 3.2 %collective-permute-done.3 = f32[8,66,1,128]{3,0,2,1:T(8,128)S(1)} collective-permute-done((f32[8,66,1,128]{3,0,2,1:T(8,128)S(1)}, f32[8,66,1,128]{3,0,2,1:T(8,128)S(1)}, u32[]{:S(2)}, u32[]{:S(2)}) %collective-permute-start.3) | collective-permute-done | bytes 270368 | tf_op jit(solution)/shard_map/ppermute | solution.py:15
  28.2 11.9 %fusion = f32[8,64,16,128]{3,0,2,1:T(8,128)S(1)} fusion(f32[8,64,16,128]{3,0,2,1:T(8,128)S(1)} %copy.15, f32[8,66,16,128]{3,0,2,1:T(8,128)} %copy-done.2, f32[8,66,1,128]{3,0,2,1:T(8,128)S(1)} %collective-permute-done.3, f32[8,66,1,128]{3,0,2,1:T(8,128)S(1)} %collective-permute-done.2, f32[8,1,16,128]{3,0,2,1:T(8,128)S(1)} %collective-permute-done.1, ...), kind=kLoop, calls=%fused_computation.4 | loop fusion | flops 18874368 | bytes 22298688 | tf_op jit(solution)/shard_map/sub | solution.py:29
  40.2 3.8 %collective-permute-start.4 = (f32[8,1,16,128]{3,0,2,1:T(8,128)S(1)}, f32[8,1,16,128]{3,0,2,1:T(8,128)S(1)}, u32[]{:S(2)}, u32[]{:S(2)}) collective-permute-start(f32[8,1,16,128]{3,0,2,1:T(8,128)S(1)} %get-tuple-element.30), channel_id=1, source_target_pairs={{8,0},{16,8},{24,16},{0,24},{9,1},{17,9},{25,17},{1,25},{10,2},{18... | collective-permute-start | bytes 196616 | tf_op jit(solution)/shard_map/ppermute | solution.py:18
  44.0 4.8 %fusion.44 = (f32[8,64,16,127]{3,0,2,1:T(8,128)}, f32[8,64,16,127]{3,0,2,1:T(8,128)}) fusion(f32[8,64,16,128]{3,0,2,1:T(8,128)S(1)} %fusion), kind=kLoop, calls=%fused_computation.88 | loop fusion | bytes 16646144 | tf_op jit(solution)/shard_map/jit(_roll_static)/slice | solution.py:27
  49.0 0.5 collective-permute-start.7
  49.4 4.9 %fusion.43 = (f32[8,64,16,1]{3,0,2,1:T(8,128)}, f32[8,64,16,1]{3,0,2,1:T(8,128)}) fusion(f32[8,64,16,128]{3,0,2,1:T(8,128)S(1)} %fusion), kind=kLoop, calls=%fused_computation.87 | loop fusion | bytes 131072 | tf_op jit(solution)/shard_map/jit(_roll_static)/slice | solution.py:27
  54.3 1.3 %collective-permute-done.6 = f32[8,66,1,128]{3,0,2,1:T(8,128)S(1)} collective-permute-done((f32[8,66,1,128]{3,0,2,1:T(8,128)S(1)}, f32[8,66,1,128]{3,0,2,1:T(8,128)S(1)}, u32[]{:S(2)}, u32[]{:S(2)}) %collective-permute-start.6) | collective-permute-done | bytes 270368 | tf_op jit(solution)/shard_map/ppermute | solution.py:18
  55.6 1.5 %collective-permute-done.7 = f32[8,66,1,128]{3,0,2,1:T(8,128)S(1)} collective-permute-done((f32[8,66,1,128]{3,0,2,1:T(8,128)S(1)}, f32[8,66,1,128]{3,0,2,1:T(8,128)S(1)}, u32[]{:S(2)}, u32[]{:S(2)}) %collective-permute-start.7) | collective-permute-done | bytes 270368 | tf_op jit(solution)/shard_map/ppermute | solution.py:15
  57.1 9.8 %fusion.1 = f32[8,64,16,128]{3,0,2,1:T(8,128)S(1)} fusion(f32[8,64,16,128]{3,0,2,1:T(8,128)S(1)} %fusion, f32[8,66,1,128]{3,0,2,1:T(8,128)S(1)} %collective-permute-done.7, f32[8,1,16,128]{3,0,2,1:T(8,128)S(1)} %collective-permute-done.4, f32[8,1,16,128]{3,0,2,1:T(8,128)S(1)} %collective-permute-done.5, f32[8,66,1,128]{3,0,2,1:T(8,128)S(1)} %collective-permute-done.6, ...), kind=kLoop, calls=%fused_computation.5 | loop fusion | flops 23068672 | bytes 17973312 | tf_op jit(solution)/shard_map/sub | solution.py:29
  67.0 3.8 %collective-permute-start.8 = (f32[8,1,16,128]{3,0,2,1:T(8,128)S(1)}, f32[8,1,16,128]{3,0,2,1:T(8,128)S(1)}, u32[]{:S(2)}, u32[]{:S(2)}) collective-permute-start(f32[8,1,16,128]{3,0,2,1:T(8,128)S(1)} %get-tuple-element.24), channel_id=1, source_target_pairs={{8,0},{16,8},{24,16},{0,24},{9,1},{17,9},{25,17},{1,25},{10,2},{18... | collective-permute-start | bytes 196616 | tf_op jit(solution)/shard_map/ppermute | solution.py:18
  70.8 4.8 %fusion.41 = (f32[8,64,16,127]{3,0,2,1:T(8,128)}, f32[8,64,16,127]{3,0,2,1:T(8,128)}) fusion(f32[8,64,16,128]{3,0,2,1:T(8,128)S(1)} %fusion.1), kind=kLoop, calls=%fused_computation.85 | loop fusion | bytes 16646144 | tf_op jit(solution)/shard_map/jit(_roll_static)/slice | solution.py:27
  75.7 1.1 collective-permute-start.10
  76.8 4.9 %fusion.40 = (f32[8,64,16,1]{3,0,2,1:T(8,128)}, f32[8,64,16,1]{3,0,2,1:T(8,128)}) fusion(f32[8,64,16,128]{3,0,2,1:T(8,128)S(1)} %fusion.1), kind=kLoop, calls=%fused_computation.84 | loop fusion | bytes 131072 | tf_op jit(solution)/shard_map/jit(_roll_static)/slice | solution.py:27
  81.7 1.5 %collective-permute-done.10 = f32[8,66,1,128]{3,0,2,1:T(8,128)S(1)} collective-permute-done((f32[8,66,1,128]{3,0,2,1:T(8,128)S(1)}, f32[8,66,1,128]{3,0,2,1:T(8,128)S(1)}, u32[]{:S(2)}, u32[]{:S(2)}) %collective-permute-start.10) | collective-permute-done | bytes 270368 | tf_op jit(solution)/shard_map/ppermute | solution.py:18
  83.2 1.3 %collective-permute-done.11 = f32[8,66,1,128]{3,0,2,1:T(8,128)S(1)} collective-permute-done((f32[8,66,1,128]{3,0,2,1:T(8,128)S(1)}, f32[8,66,1,128]{3,0,2,1:T(8,128)S(1)}, u32[]{:S(2)}, u32[]{:S(2)}) %collective-permute-start.11) | collective-permute-done | bytes 270368 | tf_op jit(solution)/shard_map/ppermute | solution.py:15
  84.4 9.8 %fusion.2 = f32[8,64,16,128]{3,0,2,1:T(8,128)S(1)} fusion(f32[8,64,16,128]{3,0,2,1:T(8,128)S(1)} %fusion.1, f32[8,66,1,128]{3,0,2,1:T(8,128)S(1)} %collective-permute-done.11, f32[8,1,16,128]{3,0,2,1:T(8,128)S(1)} %collective-permute-done.8, f32[8,1,16,128]{3,0,2,1:T(8,128)S(1)} %collective-permute-done.9, f32[8,66,1,128]{3,0,2,1:T(8,128)S(1)} %collective-permute-done.10, ...), kind=kLoop, calls=%fused_computation.6 | loop fusion | flops 23068672 | bytes 17973312 | tf_op jit(solution)/shard_map/sub | solution.py:29
  94.3 3.8 %collective-permute-start.12 = (f32[8,1,16,128]{3,0,2,1:T(8,128)S(1)}, f32[8,1,16,128]{3,0,2,1:T(8,128)S(1)}, u32[]{:S(2)}, u32[]{:S(2)}) collective-permute-start(f32[8,1,16,128]{3,0,2,1:T(8,128)S(1)} %get-tuple-element.18), channel_id=1, source_target_pairs={{8,0},{16,8},{24,16},{0,24},{9,1},{17,9},{25,17},{1,25},{10,2},{18... | collective-permute-start | bytes 196616 | tf_op jit(solution)/shard_map/ppermute | solution.py:18
  98.2 4.8 %fusion.38 = (f32[8,64,16,127]{3,0,2,1:T(8,128)}, f32[8,64,16,127]{3,0,2,1:T(8,128)}) fusion(f32[8,64,16,128]{3,0,2,1:T(8,128)S(1)} %fusion.2), kind=kLoop, calls=%fused_computation.82 | loop fusion | bytes 16646144 | tf_op jit(solution)/shard_map/jit(_roll_static)/slice | solution.py:27
  103.0 1.0 collective-permute-start.14
  104.1 4.9 %fusion.37 = (f32[8,64,16,1]{3,0,2,1:T(8,128)}, f32[8,64,16,1]{3,0,2,1:T(8,128)}) fusion(f32[8,64,16,128]{3,0,2,1:T(8,128)S(1)} %fusion.2), kind=kLoop, calls=%fused_computation.81 | loop fusion | bytes 131072 | tf_op jit(solution)/shard_map/jit(_roll_static)/slice | solution.py:27
  109.0 1.2 collective-permute-done.14
  110.2 1.7 %collective-permute-done.15 = f32[8,66,1,128]{3,0,2,1:T(8,128)S(1)} collective-permute-done((f32[8,66,1,128]{3,0,2,1:T(8,128)S(1)}, f32[8,66,1,128]{3,0,2,1:T(8,128)S(1)}, u32[]{:S(2)}, u32[]{:S(2)}) %collective-permute-start.15) | collective-permute-done | bytes 270368 | tf_op jit(solution)/shard_map/ppermute | solution.py:15
  111.9 9.8 %fusion.3 = f32[8,64,16,128]{3,0,2,1:T(8,128)S(1)} fusion(f32[8,64,16,128]{3,0,2,1:T(8,128)S(1)} %fusion.2, f32[8,66,1,128]{3,0,2,1:T(8,128)S(1)} %collective-permute-done.15, f32[8,1,16,128]{3,0,2,1:T(8,128)S(1)} %collective-permute-done.12, f32[8,1,16,128]{3,0,2,1:T(8,128)S(1)} %collective-permute-done.13, ...), kind=kLoop, calls=%fused_computation.7 | loop fusion | flops 23068672 | bytes 17973312 | tf_op jit(solution)/shard_map/sub | solution.py:29
  121.7 2.8 %copy.17 = f32[8,64,16,128]{3,2,1,0:T(8,128)} copy(f32[8,64,16,128]{3,0,2,1:T(8,128)S(1)} %fusion.3) | data formatting | bytes 8388608 | tf_op jit(solution)/shard_map/sub | solution.py:29
  (35 shorter events, 0.5 us)
Async XLA Ops:
  4.6 13.6 %collective-permute-start = (f32[8,1,16,128]{3,0,2,1:T(8,128)S(1)}, f32[8,1,16,128]{3,0,2,1:T(8,128)S(1)}, u32[]{:S(2)}, u32[]{:S(2)}) collective-permute-start(f32[8,1,16,128]{3,0,2,1:T(8,128)S(1)} %get-tuple-element.35), channel_id=1, source_target_pairs={{8,0},{16,8},{24,16},{0,24},{9,1},{17,9},{25,17},{1,25},{10,2},{18... | collective-permute-start | bytes 196616 | tf_op jit(solution)/shard_map/ppermute | solution.py:18
  9.8 6.1 %copy-start = (f32[8,64,16,128]{3,2,1,0:T(8,128)S(1)}, f32[8,64,16,128]{3,2,1,0:T(8,128)}, u32[]{:S(2)}) copy-start(f32[8,64,16,128]{3,2,1,0:T(8,128)} %param.4) | copy-start | bytes 12582916
  9.8 6.1 %collective-permute-start.1 = (f32[8,1,16,128]{3,0,2,1:T(8,128)S(1)}, f32[8,1,16,128]{3,0,2,1:T(8,128)S(1)}, u32[]{:S(2)}, u32[]{:S(2)}) collective-permute-start(f32[8,1,16,128]{3,0,2,1:T(8,128)S(1)} %get-tuple-element.36), channel_id=1, source_target_pairs={{0,8},{8,16},{16,24},{24,0},{1,9},{9,17},{17,25},{25,1},{2,10},{10... | collective-permute-start | bytes 196616 | tf_op jit(solution)/shard_map/ppermute | solution.py:15
  18.3 5.6 %copy-start.2 = (f32[8,66,16,128]{3,0,2,1:T(8,128)}, f32[8,66,16,128]{3,0,2,1:T(8,128)S(1)}, u32[]{:S(2)}) copy-start(f32[8,66,16,128]{3,0,2,1:T(8,128)S(1)} %constant_dynamic-update-slice_fusion) | copy-start | bytes 12976132
  18.4 6.6 %collective-permute-start.2 = (f32[8,66,1,128]{3,0,2,1:T(8,128)S(1)}, f32[8,66,1,128]{3,0,2,1:T(8,128)S(1)}, u32[]{:S(2)}, u32[]{:S(2)}) collective-permute-start(f32[8,66,1,128]{3,0,2,1:T(8,128)S(1)} %get-tuple-element.11), channel_id=1, source_target_pairs={{1,0},{2,1},{3,2},{4,3},{5,4},{6,5},{7,6},{0,7},{9,8},{10,9},{11,1... | collective-permute-start | bytes 811016 | tf_op jit(solution)/shard_map/ppermute | solution.py:18
  18.9 9.3 %copy-start.1 = (f32[64,16,128]{2,1,0:T(8,128)S(1)}, f32[64,16,128]{2,1,0:T(8,128)}, u32[]{:S(2)}) copy-start(f32[64,16,128]{2,1,0:T(8,128)} %param.5) | copy-start | bytes 1572868
  18.9 9.3 %copy-start.3 = (f32[8]{0:T(128)S(1)}, f32[8]{0:T(128)}, u32[]{:S(2)}) copy-start(f32[8]{0:T(128)} %param.7) | copy-start | bytes 100
  18.9 9.3 %copy-start.4 = (f32[8]{0:T(128)S(1)}, f32[8]{0:T(128)}, u32[]{:S(2)}) copy-start(f32[8]{0:T(128)} %param.6) | copy-start | bytes 100
  18.9 9.3 %collective-permute-start.3 = (f32[8,66,1,128]{3,0,2,1:T(8,128)S(1)}, f32[8,66,1,128]{3,0,2,1:T(8,128)S(1)}, u32[]{:S(2)}, u32[]{:S(2)}) collective-permute-start(f32[8,66,1,128]{3,0,2,1:T(8,128)S(1)} %get-tuple-element.12), channel_id=1, source_target_pairs={{0,1},{1,2},{2,3},{3,4},{4,5},{5,6},{6,7},{7,0},{8,9},{9,10},{10,1... | collective-permute-start | bytes 811016 | tf_op jit(solution)/shard_map/ppermute | solution.py:15
  40.1 8.7 %collective-permute-start.5 = (f32[8,1,16,128]{3,0,2,1:T(8,128)S(1)}, f32[8,1,16,128]{3,0,2,1:T(8,128)S(1)}, u32[]{:S(2)}, u32[]{:S(2)}) collective-permute-start(f32[8,1,16,128]{3,0,2,1:T(8,128)S(1)} %get-tuple-element.29), channel_id=1, source_target_pairs={{0,8},{8,16},{16,24},{24,0},{1,9},{9,17},{17,25},{25,1},{2,10},{10... | collective-permute-start | bytes 196616 | tf_op jit(solution)/shard_map/ppermute | solution.py:15
  40.2 8.6 %collective-permute-start.4 = (f32[8,1,16,128]{3,0,2,1:T(8,128)S(1)}, f32[8,1,16,128]{3,0,2,1:T(8,128)S(1)}, u32[]{:S(2)}, u32[]{:S(2)}) collective-permute-start(f32[8,1,16,128]{3,0,2,1:T(8,128)S(1)} %get-tuple-element.30), channel_id=1, source_target_pairs={{8,0},{16,8},{24,16},{0,24},{9,1},{17,9},{25,17},{1,25},{10,2},{18... | collective-permute-start | bytes 196616 | tf_op jit(solution)/shard_map/ppermute | solution.py:18
  48.9 6.8 %collective-permute-start.6 = (f32[8,66,1,128]{3,0,2,1:T(8,128)S(1)}, f32[8,66,1,128]{3,0,2,1:T(8,128)S(1)}, u32[]{:S(2)}, u32[]{:S(2)}) collective-permute-start(f32[8,66,1,128]{3,0,2,1:T(8,128)S(1)} %get-tuple-element.9), channel_id=1, source_target_pairs={{1,0},{2,1},{3,2},{4,3},{5,4},{6,5},{7,6},{0,7},{9,8},{10,9},{11,1... | collective-permute-start | bytes 811016 | tf_op jit(solution)/shard_map/ppermute | solution.py:18
  49.0 8.2 %collective-permute-start.7 = (f32[8,66,1,128]{3,0,2,1:T(8,128)S(1)}, f32[8,66,1,128]{3,0,2,1:T(8,128)S(1)}, u32[]{:S(2)}, u32[]{:S(2)}) collective-permute-start(f32[8,66,1,128]{3,0,2,1:T(8,128)S(1)} %get-tuple-element.10), channel_id=1, source_target_pairs={{0,1},{1,2},{2,3},{3,4},{4,5},{5,6},{6,7},{7,0},{8,9},{9,10},{10,1... | collective-permute-start | bytes 811016 | tf_op jit(solution)/shard_map/ppermute | solution.py:15
  66.9 8.7 %collective-permute-start.9 = (f32[8,1,16,128]{3,0,2,1:T(8,128)S(1)}, f32[8,1,16,128]{3,0,2,1:T(8,128)S(1)}, u32[]{:S(2)}, u32[]{:S(2)}) collective-permute-start(f32[8,1,16,128]{3,0,2,1:T(8,128)S(1)} %get-tuple-element.23), channel_id=1, source_target_pairs={{0,8},{8,16},{16,24},{24,0},{1,9},{9,17},{17,25},{25,1},{2,10},{10... | collective-permute-start | bytes 196616 | tf_op jit(solution)/shard_map/ppermute | solution.py:15
  67.0 8.6 %collective-permute-start.8 = (f32[8,1,16,128]{3,0,2,1:T(8,128)S(1)}, f32[8,1,16,128]{3,0,2,1:T(8,128)S(1)}, u32[]{:S(2)}, u32[]{:S(2)}) collective-permute-start(f32[8,1,16,128]{3,0,2,1:T(8,128)S(1)} %get-tuple-element.24), channel_id=1, source_target_pairs={{8,0},{16,8},{24,16},{0,24},{9,1},{17,9},{25,17},{1,25},{10,2},{18... | collective-permute-start | bytes 196616 | tf_op jit(solution)/shard_map/ppermute | solution.py:18
  75.7 7.5 %collective-permute-start.10 = (f32[8,66,1,128]{3,0,2,1:T(8,128)S(1)}, f32[8,66,1,128]{3,0,2,1:T(8,128)S(1)}, u32[]{:S(2)}, u32[]{:S(2)}) collective-permute-start(f32[8,66,1,128]{3,0,2,1:T(8,128)S(1)} %get-tuple-element.7), channel_id=1, source_target_pairs={{1,0},{2,1},{3,2},{4,3},{5,4},{6,5},{7,6},{0,7},{9,8},{10,9},{11,1... | collective-permute-start | bytes 811016 | tf_op jit(solution)/shard_map/ppermute | solution.py:18
  76.8 7.7 %collective-permute-start.11 = (f32[8,66,1,128]{3,0,2,1:T(8,128)S(1)}, f32[8,66,1,128]{3,0,2,1:T(8,128)S(1)}, u32[]{:S(2)}, u32[]{:S(2)}) collective-permute-start(f32[8,66,1,128]{3,0,2,1:T(8,128)S(1)} %get-tuple-element.8), channel_id=1, source_target_pairs={{0,1},{1,2},{2,3},{3,4},{4,5},{5,6},{6,7},{7,0},{8,9},{9,10},{10,1... | collective-permute-start | bytes 811016 | tf_op jit(solution)/shard_map/ppermute | solution.py:15
  94.3 8.7 %collective-permute-start.13 = (f32[8,1,16,128]{3,0,2,1:T(8,128)S(1)}, f32[8,1,16,128]{3,0,2,1:T(8,128)S(1)}, u32[]{:S(2)}, u32[]{:S(2)}) collective-permute-start(f32[8,1,16,128]{3,0,2,1:T(8,128)S(1)} %get-tuple-element.17), channel_id=1, source_target_pairs={{0,8},{8,16},{16,24},{24,0},{1,9},{9,17},{17,25},{25,1},{2,10},{10... | collective-permute-start | bytes 196616 | tf_op jit(solution)/shard_map/ppermute | solution.py:15
  94.3 8.6 %collective-permute-start.12 = (f32[8,1,16,128]{3,0,2,1:T(8,128)S(1)}, f32[8,1,16,128]{3,0,2,1:T(8,128)S(1)}, u32[]{:S(2)}, u32[]{:S(2)}) collective-permute-start(f32[8,1,16,128]{3,0,2,1:T(8,128)S(1)} %get-tuple-element.18), channel_id=1, source_target_pairs={{8,0},{16,8},{24,16},{0,24},{9,1},{17,9},{25,17},{1,25},{10,2},{18... | collective-permute-start | bytes 196616 | tf_op jit(solution)/shard_map/ppermute | solution.py:18
  103.0 7.2 %collective-permute-start.14 = (f32[8,66,1,128]{3,0,2,1:T(8,128)S(1)}, f32[8,66,1,128]{3,0,2,1:T(8,128)S(1)}, u32[]{:S(2)}, u32[]{:S(2)}) collective-permute-start(f32[8,66,1,128]{3,0,2,1:T(8,128)S(1)} %get-tuple-element.5), channel_id=1, source_target_pairs={{1,0},{2,1},{3,2},{4,3},{5,4},{6,5},{7,6},{0,7},{9,8},{10,9},{11,1... | collective-permute-start | bytes 811016 | tf_op jit(solution)/shard_map/ppermute | solution.py:18
  104.1 7.8 %collective-permute-start.15 = (f32[8,66,1,128]{3,0,2,1:T(8,128)S(1)}, f32[8,66,1,128]{3,0,2,1:T(8,128)S(1)}, u32[]{:S(2)}, u32[]{:S(2)}) collective-permute-start(f32[8,66,1,128]{3,0,2,1:T(8,128)S(1)} %get-tuple-element.6), channel_id=1, source_target_pairs={{0,1},{1,2},{2,3},{3,4},{4,5},{5,6},{6,7},{7,0},{8,9},{9,10},{10,1... | collective-permute-start | bytes 811016 | tf_op jit(solution)/shard_map/ppermute | solution.py:15
where the time goes:
time: 125 us; the launch traced here: 124 us
  local copies, waits for them, and re-layouts  48.9 us (39%)
  other arithmetic  41.4 us (33%)
  starting transfers between devices  19.9 us (16%)
  waiting for transfers between devices  14.1 us (11%)
    sub x4, other arithmetic, advance(): return center + diffuse * laplace - decays * inner_uptake[None] * center  41.3 us
    slice x8, local copies, waits for them, and re-layouts, advance(): laplace = laplace + jnp.roll(center, -1, 3) + jnp.roll(center, 1, 3)  38.9 us
    ppermute x8, starting transfers between devices, padded_2(): lax.ppermute(lax.slice_in_dim(block, 0, width, axis=dim), axis, backward)  19.2 us
    ppermute x8, waiting for transfers between devices, padded_2(): lax.ppermute(lax.slice_in_dim(block, block.shape[dim] - width, None, axis...  8.9 us
    unnamed x13, local copies, waits for them, and re-layouts  7.07 us
    ppermute x8, waiting for transfers between devices, padded_2(): lax.ppermute(lax.slice_in_dim(block, 0, width, axis=dim), axis, backward)  5.17 us
    sub x1, local copies, waits for them, and re-layouts, advance(): return center + diffuse * laplace - decays * inner_uptake[None] * center  2.77 us
  transfers between devices with their start and end apart: 16, of which 9 were waited for; matrix products, arithmetic and copies ran while one was open for 33% of the time, Pallas kernels for 0%

commit v1 on v0

v1 whole, which is shorter than its diff:
```python
import functools

import jax
import jax.numpy as jnp
from jax import lax
from jax.experimental import pallas as pl
from jax.experimental.pallas import tpu as pltpu
from jax.sharding import PartitionSpec as P

SUBSTEPS = 4
PITCH_PAD = 16
Y0 = 8
MESH = pl.DeviceIdType.MESH


def kernel(
    n_x, n_y, sub_ref, up_ref, dif_ref, dec_ref, out_ref,
    field, uptake, result, faces, halos, load_sem, up_sem, store_sem, send_sem, recv_sem,
):
    count, cx, cy, cz = sub_ref.shape
    pitch = cy + PITCH_PAD
    rows = field.reshape(SUBSTEPS, count, (cx + 2) * pitch, cz)
    gx, gy = lax.axis_index("gx"), lax.axis_index("gy")
    low_x, high_x = lax.rem(gx + n_x - 1, n_x), lax.rem(gx + 1, n_x)
    low_y, high_y = lax.rem(gy + n_y - 1, n_y), lax.rem(gy + 1, n_y)
    inner = pl.ds(Y0, cy)

    def load(s):
        return pltpu.make_async_copy(
            sub_ref.at[s], field.at[0, s, pl.ds(1, cx), inner, :], load_sem.at[s]
        )

    def store(s):
        return pltpu.make_async_copy(result.at[s], out_ref.at[s], store_sem.at[s])

    def sends(t, s):
        here = field.at[t, s]
        pairs = (
            (faces.at[t, s, 0], halos.at[t, s, 0], (gx, low_y)),
            (faces.at[t, s, 1], halos.at[t, s, 1], (gx, high_y)),
            (here.at[1, inner, :], here.at[cx + 1, inner, :], (low_x, gy)),
            (here.at[cx, inner, :], here.at[0, inner, :], (high_x, gy)),
        )
        return [
            pltpu.make_async_remote_copy(
                src_ref=src, dst_ref=dst, send_sem=send_sem.at[t, s, k],
                recv_sem=recv_sem.at[t, s, k], device_id=target, device_id_type=MESH,
            )
            for k, (src, dst, target) in enumerate(pairs)
        ]

    def emit(t, s):
        for i in range(cx // 8):
            top = (1 + 8 * i) * pitch + Y0
            faces[t, s, 0, pl.ds(8 * i, 8), :] = rows[t, s, pl.ds(top, 8, stride=pitch), :]
            faces[t, s, 1, pl.ds(8 * i, 8), :] = rows[
                t, s, pl.ds(top + cy - 1, 8, stride=pitch), :
            ]
        for copy in sends(t, s):
            copy.start()

    def unit(t, s):
        for copy in sends(t, s):
            copy.wait_recv()
        for i in range(cx // 8):
            top = (1 + 8 * i) * pitch + Y0
            rows[t, s, pl.ds(top + cy, 8, stride=pitch), :] = halos[t, s, 0, pl.ds(8 * i, 8), :]
            rows[t, s, pl.ds(top - 1, 8, stride=pitch), :] = halos[t, s, 1, pl.ds(8 * i, 8), :]
        diffuse = dif_ref[s]
        keep = 1.0 - 6.0 * diffuse
        decay = dec_ref[s]
        block = 8

        def strip(b, carry):
            x0 = b * block
            for y in range(0, cy, 8):
                below = field[t, s, x0, pl.ds(Y0 + y, 8), :]
                center = field[t, s, x0 + 1, pl.ds(Y0 + y, 8), :]
                for i in range(block):
                    x = x0 + i
                    above = field[t, s, x + 2, pl.ds(Y0 + y, 8), :]
                    total = below + above
                    total = total + (
                        field[t, s, x + 1, pl.ds(Y0 + y - 1, 8), :]
                        + field[t, s, x + 1, pl.ds(Y0 + y + 1, 8), :]
                    )
                    total = total + (pltpu.roll(center, 1, 1) + pltpu.roll(center, cz - 1, 1))
                    factor = keep - decay * uptake[x, pl.ds(y, 8), :]
                    value = diffuse * total + factor * center
                    if t + 1 < SUBSTEPS:
                        field[t + 1, s, x + 1, pl.ds(Y0 + y, 8), :] = value
                    else:
                        result[s, x, pl.ds(y, 8), :] = value
                    below, center = center, above
            return carry

        lax.fori_loop(0, cx // block, strip, 0)

    each = functools.partial(lax.fori_loop, 0, count, init_val=0)

    def run(body):
        def wrapped(s, carry):
            body(s)
            return carry

        each(body_fun=wrapped)

    run(lambda s: load(s).start())
    up_copy = pltpu.make_async_copy(up_ref, uptake, up_sem)
    up_copy.start()
    barrier = pltpu.get_barrier_semaphore()
    for target in ((gx, low_y), (gx, high_y), (low_x, gy), (high_x, gy)):
        pl.semaphore_signal(barrier, inc=1, device_id=target, device_id_type=MESH)
    pl.semaphore_wait(barrier, 4)

    def first(s):
        load(s).wait()
        emit(0, s)

    run(first)
    up_copy.wait()
    for t in range(SUBSTEPS):

        def advance(s):
            unit(t, s)
            if t + 1 < SUBSTEPS:
                emit(t + 1, s)
            else:
                store(s).start()

        run(advance)

    def finish(s):
        for t in range(SUBSTEPS):
            for copy in sends(t, s):
                copy.wait_send()
        store(s).wait()

    run(finish)


def solution(mesh):
    n_x, n_y = mesh.shape["gx"], mesh.shape["gy"]

    def local(substrates, uptake, diffusion, decay_rate):
        count, cx, cy, cz = substrates.shape
        any_spec = pl.BlockSpec(memory_space=pl.ANY)
        smem_spec = pl.BlockSpec(memory_space=pltpu.SMEM)
        return pl.pallas_call(
            functools.partial(kernel, n_x, n_y),
            out_shape=jax.ShapeDtypeStruct(substrates.shape, substrates.dtype),
            in_specs=[any_spec, any_spec, smem_spec, smem_spec],
            out_specs=any_spec,
            scratch_shapes=[
                pltpu.VMEM((SUBSTEPS, count, cx + 2, cy + PITCH_PAD, cz), jnp.float32),
                pltpu.VMEM((cx, cy, cz), jnp.float32),
                pltpu.VMEM((count, cx, cy, cz), jnp.float32),
                pltpu.VMEM((SUBSTEPS, count, 2, cx, cz), jnp.float32),
                pltpu.VMEM((SUBSTEPS, count, 2, cx, cz), jnp.float32),
                pltpu.SemaphoreType.DMA((count,)),
                pltpu.SemaphoreType.DMA,
                pltpu.SemaphoreType.DMA((count,)),
                pltpu.SemaphoreType.DMA((SUBSTEPS, count, 4)),
                pltpu.SemaphoreType.DMA((SUBSTEPS, count, 4)),
            ],
            compiler_params=pltpu.CompilerParams(
                collective_id=0, has_side_effects=True, vmem_limit_bytes=62 * 1024 * 1024
            ),
        )(substrates, uptake, diffusion, decay_rate)

    placed = (P(None, "gx", "gy", None), P("gx", "gy", None), P(), P())
    return jax.shard_map(
        local, mesh=mesh, in_specs=placed, out_specs=P(None, "gx", "gy", None), check_vma=False
    )
```

time: 125 us -> 47.8 us (0.38)
  local copies, waits for them, and re-layouts: 48.9 us -> 4.5 us
  Pallas kernels: 0 us -> 43.1 us
  other arithmetic: 41.4 us -> 0 us
  starting transfers between devices: 19.9 us -> 0 us
  waiting for transfers between devices: 14.1 us -> 0 us
    pallas_call x0 -> x1, Pallas kernels: none -> 43.1 us  [local(): pl.pallas_call(functools.partial(kernel, n_x, n_y), out_shape=jax.ShapeDt...]
    sub x4 -> x0, other arithmetic: 41.3 us -> none  [advance(): return center + diffuse * laplace - decays * inner_uptake[None] * center]
    slice x13 -> x0, local copies, waits for them, and re-layouts: 39 us -> none  [the longest x8 38.9 us: advance(): laplace = laplace + jnp.roll(center, -1, 3) + jnp.roll(center, 1, 3)]
    ppermute x16 -> x0, starting transfers between devices: 19.9 us -> none  [the longest x8 19.2 us: padded_2(): lax.ppermute(lax.slice_in_dim(block, 0, width, axis=dim), axis, backward)]
    ppermute x16 -> x0, waiting for transfers between devices: 14.1 us -> none  [the longest x8 8.9 us: padded_2(): lax.ppermute(lax.slice_in_dim(block, block.shape[dim] - width, None, axis...]
    sub x1 -> x0, local copies, waits for them, and re-layouts: 2.77 us -> none  [advance(): return center + diffuse * laplace - decays * inner_uptake[None] * center]
    unnamed x13 -> x1, local copies, waits for them, and re-layouts: 7.07 us -> 4.5 us
  transfers between devices with their start and end apart: 16 -> 0, of which waited for: 9 -> 0; matrix products, arithmetic and copies ran while one was open for 33% -> 0% of each run, Pallas kernels for 0% -> 0%
where the time goes in v1:
time: 47.8 us; the launch traced here: 47.6 us
  Pallas kernels  43.1 us (90%)
  local copies, waits for them, and re-layouts  4.5 us (9%)
    pallas_call x1, Pallas kernels, local(): pl.pallas_call(functools.partial(kernel, n_x, n_y), out_shape=jax.ShapeDt...  43.1 us
    unnamed x1, local copies, waits for them, and re-layouts  4.5 us

profile of v1, /device:TPU:0, one launch (start us, length us, event | category | flops | bytes accessed | tf_op | source)
XLA Modules:
  0.0 47.6 jit_solution(2684598564798208297)
XLA Ops:
  0.0 43.1 %shard_map.46 = f32[8,64,16,128]{3,2,1,0:T(8,128)} custom-call(f32[8,64,16,128]{3,2,1,0:T(8,128)} %sub_ref.1, f32[64,16,128]{2,1,0:T(8,128)} %up_ref.1, f32[8]{0:T(128)} %dif_ref.1, f32[8]{0:T(128)} %dec_ref.1), custom_call_target="tpu_custom_call" | custom-call | tf_op jit(solution)/shard_map/pallas_call | solution.py:149
  43.1 4.5 %copy.6 = f32[8,64,16,128]{3,2,1,0:T(8,128)} copy(f32[8,64,16,128]{3,2,1,0:T(8,128)} %shard_map.46) | data formatting | bytes 8388608

commit v2 on v1

--- a/solution.py
+++ b/solution.py
@@ -69,7 +69,7 @@
         diffuse = dif_ref[s]
         keep = 1.0 - 6.0 * diffuse
         decay = dec_ref[s]
-        block = 8
+        block = cx
 
         def strip(b, carry):
             x0 = b * block
@@ -145,11 +145,12 @@
     def local(substrates, uptake, diffusion, decay_rate):
         count, cx, cy, cz = substrates.shape
         any_spec = pl.BlockSpec(memory_space=pl.ANY)
+        hbm_spec = pl.BlockSpec(memory_space=pltpu.HBM)
         smem_spec = pl.BlockSpec(memory_space=pltpu.SMEM)
         return pl.pallas_call(
             functools.partial(kernel, n_x, n_y),
             out_shape=jax.ShapeDtypeStruct(substrates.shape, substrates.dtype),
-            in_specs=[any_spec, any_spec, smem_spec, smem_spec],
+            in_specs=[hbm_spec, hbm_spec, smem_spec, smem_spec],
             out_specs=any_spec,
             scratch_shapes=[
                 pltpu.VMEM((SUBSTEPS, count, cx + 2, cy + PITCH_PAD, cz), jnp.float32),
@@ -164,7 +165,7 @@
                 pltpu.SemaphoreType.DMA((SUBSTEPS, count, 4)),
             ],
             compiler_params=pltpu.CompilerParams(
-                collective_id=0, has_side_effects=True, vmem_limit_bytes=62 * 1024 * 1024
+                collective_id=0, has_side_effects=True, vmem_limit_bytes=47 * 1024 * 1024
             ),
         )(substrates, uptake, diffusion, decay_rate)
 

time: 47.8 us -> 37.6 us (0.79)
  Pallas kernels: 43.1 us -> 33 us
    pallas_call x1, Pallas kernels: 43.1 us -> 33 us  [local(): pl.pallas_call(functools.partial(kernel, n_x, n_y), out_shape=jax.ShapeDt...]
    unnamed x1 -> x7, local copies, waits for them, and re-layouts: 4.5 us -> 4.37 us
where the time goes in v2:
time: 37.6 us; the launch traced here: 37.4 us
  Pallas kernels  33 us (88%)
  local copies, waits for them, and re-layouts  4.37 us (12%)
    pallas_call x1, Pallas kernels, local(): pl.pallas_call(functools.partial(kernel, n_x, n_y), out_shape=jax.ShapeDt...  33 us
    unnamed x7, local copies, waits for them, and re-layouts  4.37 us

profile of v2, /device:TPU:0, one launch (start us, length us, event | category | flops | bytes accessed | tf_op | source)
XLA Modules:
  0.0 37.4 jit_solution(5373660401503798458)
XLA Ops:
  0.0 0.0 copy-start
  0.0 1.0 %copy-done = f32[64,16,128]{2,1,0:T(8,128)S(1)} copy-done((f32[64,16,128]{2,1,0:T(8,128)S(1)}, f32[64,16,128]{2,1,0:T(8,128)}, u32[]{:S(2)}) %copy-start) | copy-done | bytes 524312
  1.0 0.0 copy-start.1
  1.0 0.7 %copy-done.1 = f32[8]{0:T(128)S(1)} copy-done((f32[8]{0:T(128)S(1)}, f32[8]{0:T(128)}, u32[]{:S(2)}) %copy-start.1) | copy-done | bytes 56
  1.7 0.0 copy-start.2
  1.7 0.7 %copy-done.2 = f32[8]{0:T(128)S(1)} copy-done((f32[8]{0:T(128)S(1)}, f32[8]{0:T(128)}, u32[]{:S(2)}) %copy-start.2) | copy-done | bytes 56
  2.4 33.0 %shard_map.46 = f32[8,64,16,128]{3,2,1,0:T(8,128)S(1)} custom-call(f32[8,64,16,128]{3,2,1,0:T(8,128)} %sub_ref.1, f32[64,16,128]{2,1,0:T(8,128)S(1)} %copy-done, f32[8]{0:T(128)S(1)} %copy-done.1, f32[8]{0:T(128)S(1)} %copy-done.2), custom_call_target="tpu_custom_call" | custom-call | tf_op jit(solution)/shard_map/pallas_call | solution.py:150
  35.4 2.0 %copy.6 = f32[8,64,16,128]{3,2,1,0:T(8,128)} copy(f32[8,64,16,128]{3,2,1,0:T(8,128)S(1)} %shard_map.46) | data formatting | bytes 8388608
Async XLA Ops:
  0.0 1.0 %copy-start = (f32[64,16,128]{2,1,0:T(8,128)S(1)}, f32[64,16,128]{2,1,0:T(8,128)}, u32[]{:S(2)}) copy-start(f32[64,16,128]{2,1,0:T(8,128)} %up_ref.1) | copy-start | bytes 1572868
  1.0 0.7 %copy-start.1 = (f32[8]{0:T(128)S(1)}, f32[8]{0:T(128)}, u32[]{:S(2)}) copy-start(f32[8]{0:T(128)} %dif_ref.1) | copy-start | bytes 100
  1.7 0.7 %copy-start.2 = (f32[8]{0:T(128)S(1)}, f32[8]{0:T(128)}, u32[]{:S(2)}) copy-start(f32[8]{0:T(128)} %dec_ref.1) | copy-start | bytes 100

commit v3 on v2

--- a/solution.py
+++ b/solution.py
@@ -14,8 +14,9 @@
 
 
 def kernel(
-    n_x, n_y, sub_ref, up_ref, dif_ref, dec_ref, out_ref,
+    n_x, n_y, sub_ref, up_ref, dif_hbm, dec_hbm, out_ref,
     field, uptake, result, faces, halos, load_sem, up_sem, store_sem, send_sem, recv_sem,
+    dif_ref, dec_ref, scalar_sem,
 ):
     count, cx, cy, cz = sub_ref.shape
     pitch = cy + PITCH_PAD
@@ -108,6 +109,12 @@
     run(lambda s: load(s).start())
     up_copy = pltpu.make_async_copy(up_ref, uptake, up_sem)
     up_copy.start()
+    scalar_copies = [
+        pltpu.make_async_copy(dif_hbm, dif_ref, scalar_sem.at[0]),
+        pltpu.make_async_copy(dec_hbm, dec_ref, scalar_sem.at[1]),
+    ]
+    for copy in scalar_copies:
+        copy.start()
     barrier = pltpu.get_barrier_semaphore()
     for target in ((gx, low_y), (gx, high_y), (low_x, gy), (high_x, gy)):
         pl.semaphore_signal(barrier, inc=1, device_id=target, device_id_type=MESH)
@@ -119,6 +126,8 @@
 
     run(first)
     up_copy.wait()
+    for copy in scalar_copies:
+        copy.wait()
     for t in range(SUBSTEPS):
 
         def advance(s):
@@ -146,11 +155,10 @@
         count, cx, cy, cz = substrates.shape
         any_spec = pl.BlockSpec(memory_space=pl.ANY)
         hbm_spec = pl.BlockSpec(memory_space=pltpu.HBM)
-        smem_spec = pl.BlockSpec(memory_space=pltpu.SMEM)
         return pl.pallas_call(
             functools.partial(kernel, n_x, n_y),
             out_shape=jax.ShapeDtypeStruct(substrates.shape, substrates.dtype),
-            in_specs=[hbm_spec, hbm_spec, smem_spec, smem_spec],
+            in_specs=[hbm_spec] * 4,
             out_specs=any_spec,
             scratch_shapes=[
                 pltpu.VMEM((SUBSTEPS, count, cx + 2, cy + PITCH_PAD, cz), jnp.float32),
@@ -163,11 +171,14 @@
                 pltpu.SemaphoreType.DMA((count,)),
                 pltpu.SemaphoreType.DMA((SUBSTEPS, count, 4)),
                 pltpu.SemaphoreType.DMA((SUBSTEPS, count, 4)),
+                pltpu.SMEM((count,), jnp.float32),
+                pltpu.SMEM((count,), jnp.float32),
+                pltpu.SemaphoreType.DMA((2,)),
             ],
             compiler_params=pltpu.CompilerParams(
                 collective_id=0, has_side_effects=True, vmem_limit_bytes=47 * 1024 * 1024
             ),
-        )(substrates, uptake, diffusion, decay_rate)
+        )(*[pltpu.with_memory_space_constraint(v, pltpu.HBM) for v in (substrates, uptake, diffusion, decay_rate)])
 
     placed = (P(None, "gx", "gy", None), P("gx", "gy", None), P(), P())
     return jax.shard_map(

time: 37.6 us -> 34.6 us (0.920)
  local copies, waits for them, and re-layouts: 4.37 us -> 2.02 us
  Pallas kernels: 33 us -> 32.4 us
    unnamed x7 -> x1, local copies, waits for them, and re-layouts: 4.37 us -> 2.02 us
    pallas_call x1, Pallas kernels: 33 us -> 32.4 us  [local(): pl.pallas_call(functools.partial(kernel, n_x, n_y), out_shape=jax.ShapeDt...]
where the time goes in v3:
time: 34.6 us; the launch traced here: 34.4 us
  Pallas kernels  32.4 us (94%)
  local copies, waits for them, and re-layouts  2.02 us (6%)
    pallas_call x1, Pallas kernels, local(): pl.pallas_call(functools.partial(kernel, n_x, n_y), out_shape=jax.ShapeDt...  32.4 us
    unnamed x1, local copies, waits for them, and re-layouts  2.02 us

profile of v3, /device:TPU:0, one launch (start us, length us, event | category | flops | bytes accessed | tf_op | source)
XLA Modules:
  0.0 34.4 jit_solution(11738133498252034431)
XLA Ops:
  0.0 32.4 %shard_map.46 = f32[8,64,16,128]{3,2,1,0:T(8,128)S(1)} custom-call(f32[8,64,16,128]{3,2,1,0:T(8,128)} %sub_ref.1, f32[64,16,128]{2,1,0:T(8,128)} %up_ref.1, f32[8]{0:T(128)} %dif_hbm.1, f32[8]{0:T(128)} %dec_hbm.1), custom_call_target="tpu_custom_call" | custom-call | tf_op jit(solution)/shard_map/pallas_call | solution.py:158
  32.4 2.0 %copy.6 = f32[8,64,16,128]{3,2,1,0:T(8,128)} copy(f32[8,64,16,128]{3,2,1,0:T(8,128)S(1)} %shard_map.46) | data formatting | bytes 8388608
